TPU v7x, 32 devices: a whole 2x2x4 slice. The times are simulated.
32 devices in a mesh: dp: 4 (over y, x), row: 2 (over core), col: 4 (over z).
Axes of the slice: x: 2, y: 2, z: 4, core: 2. Of those that a mesh axis runs over, the one named last changes fastest.
Arguments:
- tokens: bfloat16 [3840, 4096], P(('dp', 'col'), 'row'), may hold values from -6 to 6
- hidden_cot: bfloat16 [3840, 14336], P(('dp', 'row'), 'col'), may hold values from -0.09667969 to 0.09667969
- gate_pre: bfloat16 [3840, 14336], P(('dp', 'row'), 'col'), may hold values from -10 to 10
- up_pre: bfloat16 [3840, 14336], P(('dp', 'row'), 'col'), may hold values from -6 to 6
Outputs:
- grad_gate: bfloat16 [2, 2048, 14336], P('row', 'dp', 'col')
All inputs are finite; a program needn't handle non-finite values.
Results may differ from a plain program's by a relative error of at most 0.014.
Values may be sent and summed in bfloat16 or wider, within the bound.
No kernel may reach another device: no remote copies, remote signals or barrier semaphores. Data moves between devices by JAX's collectives and lax.ppermute only.
A program may use at most 128 MiB of HBM per device.

v0:
```python
import jax
import jax.numpy as jnp
from jax import lax
from jax.sharding import PartitionSpec as P


def contract_rows(left, right):
    return lax.dot_general(
        left, right, (((0,), (0,)), ((), ())), preferred_element_type=jnp.float32
    )


def on_device(tokens, hidden_cot, gate_pre, up_pre):
    tok_full = lax.all_gather(tokens, "col", axis=0, tiled=True)
    gate_val = gate_pre.astype(jnp.float32)
    up_val = up_pre.astype(jnp.float32)
    cot_val = hidden_cot.astype(jnp.float32)
    sigma = jax.nn.sigmoid(gate_val)
    gate_grad = (cot_val * up_val * sigma * (1.0 + gate_val * (1.0 - sigma))).astype(jnp.bfloat16)
    grad_full = lax.all_gather(gate_grad, "row", axis=0, tiled=True)
    group_part = contract_rows(tok_full, grad_full)
    summed = lax.psum_scatter(
        group_part.astype(jnp.bfloat16), "dp", scatter_dimension=0, tiled=True
    )
    return summed.reshape(1, summed.shape[0], summed.shape[1])


def solution(mesh):
    in_specs = (
        P(("dp", "col"), "row"),
        P(("dp", "row"), "col"),
        P(("dp", "row"), "col"),
        P(("dp", "row"), "col"),
    )
    out_specs = P("row", "dp", "col")
    return jax.shard_map(
        on_device, mesh=mesh, in_specs=in_specs, out_specs=out_specs, check_vma=False
    )
```

profile of v0, /device:TPU:0, one launch (start us, length us, event | category | flops | bytes accessed | tf_op | source)
XLA Modules:
  0.0 279.2 jit_solution(14229257457182751783)
XLA Ops:
  6.5 0.0 all-gather.5.cloned.1.call-start
  6.5 0.7 all-gather.5.cloned.1.call-update
  7.3 0.0 all-gather.3.cloned.1.call-start
  7.3 6.7 %fusion.6 = bf16[480,3584]{1,0:T(8,128)(2,1)} fusion(bf16[480,3584]{1,0:T(8,128)(2,1)} %param.6, bf16[480,3584]{1,0:T(8,128)(2,1)} %param.7, bf16[480,3584]{1,0:T(8,128)(2,1)} %param.5), kind=kLoop, calls=%fused_computation.9 | loop fusion | flops 22364160 | bytes 13762560 | tf_op jit(solution)/shard_map/convert_element_type | solution.py:19
  14.0 0.0 all-gather.3.cloned.1.call-update
  14.1 0.0 reduce-scatter.2.cloned.1.call-start
  14.1 74.0 %all-gather.5.cloned.1.call-done = bf16[960,2048]{1,0:T(8,128)(2,1)} async-done(((bf16[240,2048]{1,0:T(8,128)(2,1)}), bf16[960,2048]{1,0:T(8,128)(2,1)}) %all-gather.5.cloned.1.call-update) | async-done | bytes 3932176 | tf_op jit(solution)/shard_map/all_gather | solution.py:14
  88.1 17.7 %all-gather.3.cloned.1.call-done = bf16[960,3584]{1,0:T(8,128)(2,1)} async-done(((bf16[480,3584]{1,0:T(8,128)(2,1)}), bf16[960,3584]{1,0:T(8,128)(2,1)}) %all-gather.3.cloned.1.call-update) | async-done | bytes 6881296 | tf_op jit(solution)/shard_map/all_gather | solution.py:20
  105.8 21.9 %fusion = bf16[2048,3584]{0,1:T(8,128)(2,1)} fusion(bf16[960,3584]{1,0:T(8,128)(2,1)} %all-gather.3.cloned.1.call-done, bf16[960,2048]{1,0:T(8,128)(2,1)} %all-gather.5.cloned.1.call-done), kind=kOutput, calls=%fused_computation.1 | convolution fusion | flops 14100201472 | bytes 25493504 | tf_op jit(solution)/shard_map/dot_general | solution.py:8
  127.7 0.0 reduce-scatter.2.cloned.1.call-update
  127.7 139.1 %reduce-scatter.2.cloned.1.call-done = bf16[512,3584]{0,1:T(8,128)(2,1)} async-done(((bf16[2048,3584]{0,1:T(8,128)(2,1)}), bf16[512,3584]{0,1:T(8,128)(2,1)}) %reduce-scatter.2.cloned.1.call-update) | async-done | bytes 3670032 | tf_op jit(solution)/shard_map/reduce_scatter | solution.py:22
  266.8 5.9 %copy.5 = bf16[1,512,3584]{2,1,0:T(8,128)(2,1)} copy(bf16[1,512,3584]{1,2,0:T(8,128)(2,1)} %bitcast.5) | data formatting | bytes 7340032 | tf_op jit(solution)/shard_map/reshape | solution.py:25
Async XLA Ops:
  6.5 81.5 %all-gather.5.cloned.1.call-start = ((), (), s32[]{:S(2)}) async-start(), calls=%async_computation.2 | async-start | bytes 4915200 | tf_op jit(solution)/shard_map/all_gather | solution.py:14
  7.3 98.5 %all-gather.3.cloned.1.call-start = ((), (), s32[]{:S(2)}) async-start(), calls=%async_computation.1 | async-start | bytes 10321920 | tf_op jit(solution)/shard_map/all_gather | solution.py:20
  14.1 252.7 %reduce-scatter.2.cloned.1.call-start = ((), (), s32[]{:S(2)}) async-start(), calls=%async_computation.3 | async-start | bytes 18350080 | tf_op jit(solution)/shard_map/reduce_scatter | solution.py:22
Sparse Core Ops, SparseCore 0:
  8.9 79.1 all-gather.4
  89.6 16.1 all-gather.2
  127.8 138.9 reduce-scatter.1
where the time goes:
time: 279 us
  waiting for transfers between devices  232 us (83%)
  matrix products  21.9 us (8%)
  between operations  13.1 us (5%)
  other arithmetic  6.73 us (2%)
  local copies, waits for them, and re-layouts  5.91 us (2%)
    reduce_scatter x1, waiting for transfers between devices, on_device(): lax.psum_scatter(group_part.astype(jnp.bfloat16), 'dp', scatter_dimension...  139 us
    all_gather x1, waiting for transfers between devices, on_device(): tok_full = lax.all_gather(tokens, 'col', axis=0, tiled=True)  74 us
    dot_general x1, matrix products, contract_rows(): lax.dot_general(left, right, (((0,), (0,)), ((), ())), preferred_element_...  21.9 us
    all_gather x1, waiting for transfers between devices, on_device(): grad_full = lax.all_gather(gate_grad, 'row', axis=0, tiled=True)  17.7 us
    convert_element_type x1, other arithmetic, on_device(): (cot_val * up_val * sigma * (1.0 + gate_val * (1.0 - sigma))).astype(jnp....  6.73 us
    reshape x1, local copies, waits for them, and re-layouts, on_device(): return summed.reshape(1, summed.shape[0], summed.shape[1])  5.91 us
  transfers between devices with their start and end apart: 3, of which 3 were waited for; matrix products, arithmetic and copies ran while one was open for 2% of the time, Pallas kernels for 0%

commit v1 on v0

v1 whole, which is shorter than its diff:
```python
import functools
import math

import jax
import jax.numpy as jnp
from jax import lax
from jax.experimental import pallas as pl
from jax.experimental.pallas import tpu as pltpu
from jax.sharding import PartitionSpec as P


CHUNKS = 7
BLOCK = 256
ANY = pl.ANY


def room(*parts):
    return pltpu.CompilerParams(vmem_limit_bytes=sum(math.prod(p) for p in parts) + (3 << 20))


def split(width, parts):
    units = width // 128
    cuts = [units * i // parts * 128 for i in range(parts)] + [width]
    return [(a, b - a) for a, b in zip(cuts, cuts[1:]) if b > a]


def assemble(nz, offsets, *refs):
    place, shards, out, held, sems = refs[0], refs[1:-3], refs[-3], refs[-2], refs[-1]
    size = shards[0].shape[0]
    copies = []
    for i, ref in enumerate(shards):
        group, slot = divmod(i, nz)
        start = pl.multiple_of((group * nz + (place[0] ^ offsets[slot] ^ (place[1] * (nz // 2)))) * size, 16)
        copies.append(pltpu.make_async_copy(ref, held.at[pl.ds(start, size)], sems.at[i]))
        copies[-1].start()
    for copy in copies:
        copy.wait()
    out[...] = held[...].T


def transposed(place, shards, nz, offsets):
    size, tile = shards[0].shape
    total = len(shards) * size
    return pl.pallas_call(
        functools.partial(assemble, nz, offsets),
        out_shape=jax.ShapeDtypeStruct((tile, total), jnp.bfloat16),
        in_specs=[pl.BlockSpec(memory_space=pltpu.SMEM)] + [pl.BlockSpec(memory_space=ANY)] * len(shards),
        out_specs=pl.BlockSpec(memory_space=pltpu.VMEM),
        scratch_shapes=[
            pltpu.VMEM((total, tile), jnp.bfloat16),
            pltpu.SemaphoreType.DMA((len(shards),)),
        ],
        compiler_params=room((total, tile, 6)),
        name="assemble",
    )(place, *shards)


def product(tok, grads, cols, part):
    rows = [ref[:, pl.ds(c + part.start, part.size)] for ref, c in zip(grads, cols)]
    return jnp.dot(tok[...], jnp.concatenate(rows, axis=0), preferred_element_type=jnp.float32)


def parts(width):
    return [pl.ds(c, min(BLOCK, width - c)) for c in range(0, width, BLOCK)]


def send_part(cols, width, tok, *refs):
    *grads, out, value, sems = refs
    stores = []
    for i, part in enumerate(parts(width)):
        value[:, part] = product(tok, grads, cols, part).astype(jnp.bfloat16)
        stores.append(pltpu.make_async_copy(value.at[:, part], out.at[:, part], sems.at[i]))
        stores[-1].start()
    for store in stores:
        store.wait()


def keep_part(cols, col, width, first, tok, *refs):
    *given, out, value, sems = refs
    n = len(cols)
    grads, came = given[:n], given[n:] if first else given[n:-1]
    stores = []
    for i, part in enumerate(parts(width)):
        total = product(tok, grads, cols, part)
        for ref in came:
            total = total + ref[:, part].astype(jnp.float32)
        value[:, part] = total.astype(jnp.bfloat16)
        stores.append(
            pltpu.make_async_copy(
                value.at[:, part], out.at[:, pl.ds(col + part.start, part.size)], sems.at[i]
            )
        )
        stores[-1].start()
    for store in stores:
        store.wait()


def cost(tile, total, width):
    return pl.CostEstimate(
        flops=2 * tile * total * width, bytes_accessed=2 * total * width, transcendentals=0
    )


def send_call(tok, grads, width):
    tile, total = tok.shape
    arrays, cols = zip(*grads)
    return pl.pallas_call(
        functools.partial(send_part, cols, width),
        out_shape=pltpu.HBM((tile, width), jnp.bfloat16),
        in_specs=[pl.BlockSpec(memory_space=pltpu.VMEM)] * (1 + len(arrays)),
        out_specs=pl.BlockSpec(memory_space=pltpu.HBM),
        scratch_shapes=[
            pltpu.VMEM((tile, width), jnp.bfloat16),
            pltpu.SemaphoreType.DMA((-(-width // BLOCK),)),
        ],
        cost_estimate=cost(tile, total, width),
        compiler_params=room((total, width, 4), (tile, total, 2), (tile, width, 8)),
        name="send_part",
    )(tok, *arrays)


def keep_call(tok, grads, came, out, col, width, whole):
    tile, total = tok.shape
    arrays, cols = zip(*grads)
    first = out is None
    given = [tok, *arrays, *came] + ([] if first else [out])
    return pl.pallas_call(
        functools.partial(keep_part, cols, col, width, first),
        out_shape=jax.ShapeDtypeStruct((tile, whole), jnp.bfloat16),
        in_specs=[pl.BlockSpec(memory_space=pltpu.VMEM)] * (1 + len(arrays) + len(came))
        + ([] if first else [pl.BlockSpec(memory_space=ANY)]),
        out_specs=pl.BlockSpec(memory_space=ANY),
        input_output_aliases={} if first else {len(given) - 1: 0},
        scratch_shapes=[
            pltpu.VMEM((tile, width), jnp.bfloat16),
            pltpu.SemaphoreType.DMA((-(-width // BLOCK),)),
        ],
        cost_estimate=cost(tile, total, width),
        compiler_params=room((total, width, 4), (tile, total, 2), (tile, width, 8 + 4 * len(came))),
        name="keep_part",
    )(*given)


def cotangents(cuts, *refs):
    ins, outs, whole = refs[:3], refs[3 : 3 + len(cuts)], refs[3 + len(cuts)]
    held, made, sems, done = refs[4 + len(cuts) :]
    rows = held.shape[2]

    def fetch(j):
        col, width = cuts[j]
        return [
            pltpu.make_async_copy(
                ins[i].at[:, pl.ds(col, width)], held.at[j % 2, i, :, pl.ds(0, width)], sems.at[j % 2, i]
            )
            for i in range(3)
        ]

    def store(j):
        col, width = cuts[j]
        value = made.at[j % 2, :, pl.ds(0, width)]
        return [
            pltpu.make_async_copy(value, outs[j], done.at[j % 2, 0]),
            pltpu.make_async_copy(value, whole.at[:, pl.ds(col - cuts[0][0], width)], done.at[j % 2, 1]),
        ]

    for copy in fetch(0):
        copy.start()
    for j in range(len(cuts)):
        if j + 1 < len(cuts):
            for copy in fetch(j + 1):
                copy.start()
        for copy in fetch(j):
            copy.wait()
        if j >= 2:
            for copy in store(j - 2):
                copy.wait()
        width = cuts[j][1]

        def step(i, _, j=j, width=width):
            part = (pl.ds(pl.multiple_of(i * 32, 32), 32), pl.ds(0, width))
            made[(j % 2, *part)] = gate_cotangent(*(held[(j % 2, n, *part)] for n in range(3)))
            return _

        lax.fori_loop(0, rows // 32, step, 0)
        for copy in store(j):
            copy.start()
    for j in range(max(0, len(cuts) - 2), len(cuts)):
        for copy in store(j):
            copy.wait()


def cotangent_call(arrays, cuts):
    rows = arrays[0].shape[0]
    wide = max(w for _, w in cuts)
    return pl.pallas_call(
        functools.partial(cotangents, cuts),
        out_shape=[pltpu.HBM((rows, w), jnp.bfloat16) for _, w in cuts]
        + [pltpu.HBM((rows, sum(w for _, w in cuts)), jnp.bfloat16)],
        in_specs=[pl.BlockSpec(memory_space=pltpu.HBM)] * 3,
        out_specs=[pl.BlockSpec(memory_space=pltpu.HBM)] * (len(cuts) + 1),
        scratch_shapes=[
            pltpu.VMEM((2, 3, rows, wide), jnp.bfloat16),
            pltpu.VMEM((2, rows, wide), jnp.bfloat16),
            pltpu.SemaphoreType.DMA((2, 3)),
            pltpu.SemaphoreType.DMA((2, 2)),
        ],
        cost_estimate=pl.CostEstimate(flops=20 * rows * wide, bytes_accessed=8 * rows * wide, transcendentals=0),
        compiler_params=room((8, rows, wide, 2)),
        name="cotangents",
    )(*arrays)


def gate_cotangent(hidden_cot, gate_pre, up_pre):
    gate_val = gate_pre.astype(jnp.float32)
    up_val = up_pre.astype(jnp.float32)
    cot_val = hidden_cot.astype(jnp.float32)
    sigma = jax.nn.sigmoid(gate_val)
    return (cot_val * up_val * sigma * (1.0 + gate_val * (1.0 - sigma))).astype(jnp.bfloat16)


def sizes_of(mesh):
    sizes = dict(mesh.shape)
    nx = math.isqrt(sizes["dp"])
    return sizes["dp"] // nx, nx, sizes["row"], sizes["col"]


def on_device(sizes, tokens, hidden_cot, gate_pre, up_pre):
    ny, nx, nrow, nz = sizes
    dp, row, z = lax.axis_index("dp"), lax.axis_index("row"), lax.axis_index("col")
    my_y, my_x = dp // nx, dp % nx
    place = jnp.stack([z, row]).astype(jnp.int32)
    tile = tokens.shape[1] // (ny * nx)
    hidden = hidden_cot.shape[1]

    def over_y(value, k):
        pairs = [(y * nx + x, (y + k) % ny * nx + x) for y in range(ny) for x in range(nx)]
        return lax.ppermute(value, "dp", pairs)

    def over_x(value, m):
        pairs = [(y * nx + x, y * nx + (x + m) % nx) for y in range(ny) for x in range(nx)]
        return lax.ppermute(value, "dp", pairs)

    def over_core(value):
        return lax.ppermute(value, "row", [(i, i ^ 1) for i in range(nrow)])

    def over_z(value):
        slots = {0: value}
        bit = nz // 2
        while bit:
            for s in list(slots):
                slots[s | bit] = lax.ppermute(slots[s], "col", [(i, i ^ bit) for i in range(nz)])
            bit //= 2
        return slots

    def columns(k, m):
        start = ((my_y + k) % ny * nx + (my_x + m) % nx) * tile
        return lax.dynamic_slice(tokens, (0, start), (tokens.shape[0], tile))

    def gathered(m):
        shards, order = [], None
        for k in range(ny):
            mine = columns(k, m)
            slots = over_z(over_y(mine, k) if k else mine)
            order = sorted(slots)
            shards += [slots[s] for s in order]
        return transposed(place, shards, nz, order)

    cuts = split(hidden, CHUNKS)
    arrays = [
        pltpu.with_memory_space_constraint(a, pltpu.HBM) for a in (hidden_cot, gate_pre, up_pre)
    ]
    own, wholes = [], []
    for part in (cuts[:1], cuts[1:]):
        *chunks, whole = cotangent_call(arrays, part)
        own += chunks
        wholes.append((whole, over_core(whole), part[0][0]))
    toks = {m: gathered(m) for m in [*range(1, nx), 0]}
    grads = []
    for j, (c, w) in enumerate(cuts):
        mine, theirs, base = wholes[j > 0]
        pieces = [(mine, c - base), (theirs, c - base)]
        for k in range(1, ny):
            held = over_y(own[j], k)
            pieces += [(held, 0), (over_core(held), 0)]
        grads.append(pieces)
    came = []
    for j, (c, w) in enumerate(cuts):
        came.append([])
        for m in range(1, nx):
            value = send_call(toks[m], grads[j], w)
            came[-1].append(over_x(value, m))
    out = None
    for j, (c, w) in enumerate(cuts):
        out = keep_call(toks[0], grads[j], came[j], out, c, w, hidden)
    return out.reshape(1, *out.shape)


def solution(mesh):
    sizes = sizes_of(mesh)

    def body(*args):
        return on_device(sizes, *args)

    return jax.shard_map(
        body,
        mesh=mesh,
        in_specs=(
            P(("dp", "col"), "row"),
            P(("dp", "row"), "col"),
            P(("dp", "row"), "col"),
            P(("dp", "row"), "col"),
        ),
        out_specs=P("row", "dp", "col"),
        check_vma=False,
    )
```

time: 279 us -> 232 us (0.83)
  waiting for transfers between devices: 232 us -> 122 us
  Pallas kernels: 0 us -> 57.4 us
  starting transfers between devices: 0.08 us -> 31.3 us
  matrix products: 21.9 us -> 0 us
  local copies, waits for them, and re-layouts: 5.91 us -> 19.9 us
  between operations: 13.1 us -> 0.68 us
  other arithmetic: 6.73 us -> 0.08 us
    reduce_scatter x1 -> x0, waiting for transfers between devices: 139 us -> none  [on_device(): lax.psum_scatter(group_part.astype(jnp.bfloat16), 'dp', scatter_dimension...]
    ppermute x0 -> x37, waiting for transfers between devices: none -> 122 us  [the longest x9 46 us: over_y(): return lax.ppermute(value, 'dp', pairs)]
    all_gather x2 -> x0, waiting for transfers between devices: 91.7 us -> none  [the longest x1 74 us: on_device(): tok_full = lax.all_gather(tokens, 'col', axis=0, tiled=True)]
    pallas_call x0 -> x18, Pallas kernels: none -> 57.4 us  [the longest x7 19.3 us: send_call(): pl.pallas_call(functools.partial(send_part, cols, width), out_shape=pltpu...]
    ppermute x0 -> x37, starting transfers between devices: none -> 31.3 us  [the longest x12 13.6 us: over_z(): lax.ppermute(slots[s], 'col', [(i, i ^ bit) for i in range(nz)])]
    dot_general x1 -> x0, matrix products: 21.9 us -> none  [contract_rows(): lax.dot_general(left, right, (((0,), (0,)), ((), ())), preferred_element_...]
    unnamed x0 -> x100, local copies, waits for them, and re-layouts: none -> 18.6 us
    convert_element_type x1 -> x0, other arithmetic: 6.73 us -> none  [on_device(): (cot_val * up_val * sigma * (1.0 + gate_val * (1.0 - sigma))).astype(jnp....]
  transfers between devices with their start and end apart: 3 -> 37, of which waited for: 3 -> 21; matrix products, arithmetic and copies ran while one was open for 2% -> 1% of each run, Pallas kernels for 0% -> 20%
where the time goes in v1:
time: 232 us
  waiting for transfers between devices  122 us (53%)
  Pallas kernels  57.4 us (25%)
  starting transfers between devices  31.3 us (13%)
  local copies, waits for them, and re-layouts  19.9 us (9%)
    ppermute x9, waiting for transfers between devices, over_y(): return lax.ppermute(value, 'dp', pairs)  46 us
    ppermute x12, waiting for transfers between devices, over_z(): lax.ppermute(slots[s], 'col', [(i, i ^ bit) for i in range(nz)])  41.1 us
    ppermute x7, waiting for transfers between devices, over_x(): return lax.ppermute(value, 'dp', pairs)  35.2 us
    pallas_call x7, Pallas kernels, send_call(): pl.pallas_call(functools.partial(send_part, cols, width), out_shape=pltpu...  19.3 us
    pallas_call x7, Pallas kernels, keep_call(): pl.pallas_call(functools.partial(keep_part, cols, col, width, first), out...  19.1 us
    unnamed x100, local copies, waits for them, and re-layouts  18.6 us
    ppermute x12, starting transfers between devices, over_z(): lax.ppermute(slots[s], 'col', [(i, i ^ bit) for i in range(nz)])  13.6 us
    pallas_call x2, Pallas kernels, cotangent_call(): pl.pallas_call(functools.partial(cotangents, cuts), out_shape=[pltpu.HBM(...  11.4 us
  transfers between devices with their start and end apart: 37, of which 21 were waited for; matrix products, arithmetic and copies ran while one was open for 1% of the time, Pallas kernels for 20%

profile of v1, /device:TPU:0, one launch (start us, length us, event | category | flops | bytes accessed | tf_op | source)
XLA Modules:
  0.0 231.7 jit_solution(3061559660998098245)
XLA Ops:
  0.0 8.5 %cotangents.2 = (bf16[480,512]{1,0:T(8,128)(2,1)}, bf16[480,512]{1,0:T(8,128)(2,1)}, bf16[480,512]{1,0:T(8,128)(2,1)}, bf16[480,512]{1,0:T(8,128)(2,1)}, bf16[48...) custom-call(bf16[480,3584]{1,0:T(8,128)(2,1)} %refs_0_.3, bf16[480,3584]{1,0:T(8,128)(2,1)} %refs_1_.3, ...), custom_call_target="tpu_custom_call" | custom-call | flops 4915200 | bytes 1966080 | tf_op jit(solution)/shard_map/cotangents/pallas_call | solution.py:195
  10.4 2.7 %collective-permute-start.13 = (bf16[240,512]{1,0:T(8,128)(2,1)S(1)}, bf16[240,512]{1,0:T(8,128)(2,1)S(1)}, u32[]{:S(2)}, u32[]{:S(2)}) collective-permute-start(bf16[240,512]{1,0:T(8,128)(2,1)S(1)} %get-tuple-element.23), channel_id=1, source_target_pairs={{0,16},{8,24},{16,0},{24,8},{1,17},{9,25},{17,1},{25,9},{2,18},{10... | collective-permute-start | bytes 737288 | tf_op jit(solution)/shard_map/ppermute | solution.py:237
  13.1 2.6 %collective-permute-start.11 = (bf16[240,512]{1,0:T(8,128)(2,1)S(1)}, bf16[240,512]{1,0:T(8,128)(2,1)S(1)}, u32[]{:S(2)}, u32[]{:S(2)}) collective-permute-start(bf16[240,512]{1,0:T(8,128)(2,1)S(1)} %get-tuple-element.26.refs_1_), channel_id=1, source_target_pairs={{0,2},{1,3},{2,0},{3,1},{4,6},{5,7},{6,4},{7,5},{8,10},{9,11},{10,... | collective-permute-start | bytes 737288 | tf_op jit(solution)/shard_map/ppermute | solution.py:251
  15.7 1.6 collective-permute-start.10
  17.8 2.0 collective-permute-done.13.refs_5_
  19.9 3.3 %collective-permute-start.1 = (bf16[240,512]{1,0:T(8,128)(2,1)S(1)}, bf16[240,512]{1,0:T(8,128)(2,1)S(1)}, u32[]{:S(2)}, u32[]{:S(2)}) collective-permute-start(bf16[240,512]{1,0:T(8,128)(2,1)S(1)} %get-tuple-element.25.refs_1_), channel_id=1, source_target_pairs={{0,2},{1,3},{2,0},{3,1},{4,6},{5,7},{6,4},{7,5},{8,10},{9,11},{10,... | collective-permute-start | bytes 737288 | tf_op jit(solution)/shard_map/ppermute | solution.py:251
  23.1 5.7 %collective-permute-done.11.refs_3_ = bf16[240,512]{1,0:T(8,128)(2,1)S(1)} collective-permute-done((bf16[240,512]{1,0:T(8,128)(2,1)S(1)}, bf16[240,512]{1,0:T(8,128)(2,1)S(1)}, u32[]{:S(2)}, u32[]{:S(2)}) %collective-permute-start.11) | collective-permute-done | bytes 245792 | tf_op jit(solution)/shard_map/ppermute | solution.py:251
  29.6 3.4 %collective-permute-start.15 = (bf16[240,512]{1,0:T(8,128)(2,1)S(1)}, bf16[240,512]{1,0:T(8,128)(2,1)S(1)}, u32[]{:S(2)}, u32[]{:S(2)}) collective-permute-start(bf16[240,512]{1,0:T(8,128)(2,1)S(1)} %collective-permute-done.13.refs_5_), channel_id=1, source_target_pairs={{0,2},{1,3},{2,0},{3,1},{4,6},{5,7},{6,4},{7,5},{8,10},{9,11},{10,... | collective-permute-start | bytes 737288 | tf_op jit(solution)/shard_map/ppermute | solution.py:251
  32.9 2.9 %cotangents.3 = (bf16[480,512]{1,0:T(8,128)(2,1)}, bf16[480,512]{1,0:T(8,128)(2,1)}) custom-call(bf16[480,3584]{1,0:T(8,128)(2,1)} %refs_0_.3, bf16[480,3584]{1,0:T(8,128)(2,1)} %refs_1_.3, bf16[480,3584]{1,0:T(8,128)(2,1)} %refs_2_.3), custom_call_target="tpu_custom_call" | custom-call | flops 4915200 | bytes 1966080 | tf_op jit(solution)/shard_map/cotangents/pallas_call | solution.py:195
  36.5 3.0 %collective-permute-done.1.refs_3_ = bf16[240,512]{1,0:T(8,128)(2,1)S(1)} collective-permute-done((bf16[240,512]{1,0:T(8,128)(2,1)S(1)}, bf16[240,512]{1,0:T(8,128)(2,1)S(1)}, u32[]{:S(2)}, u32[]{:S(2)}) %collective-permute-start.1) | collective-permute-done | bytes 245792 | tf_op jit(solution)/shard_map/ppermute | solution.py:251
  41.1 7.4 %collective-permute-done.15.refs_7_ = bf16[240,512]{1,0:T(8,128)(2,1)S(1)} collective-permute-done((bf16[240,512]{1,0:T(8,128)(2,1)S(1)}, bf16[240,512]{1,0:T(8,128)(2,1)S(1)}, u32[]{:S(2)}, u32[]{:S(2)}) %collective-permute-start.15) | collective-permute-done | bytes 245792 | tf_op jit(solution)/shard_map/ppermute | solution.py:251
  49.1 4.7 %collective-permute-done.12.refs_4_ = bf16[240,512]{1,0:T(8,128)(2,1)S(1)} collective-permute-done((bf16[240,512]{1,0:T(8,128)(2,1)S(1)}, bf16[240,512]{1,0:T(8,128)(2,1)S(1)}, u32[]{:S(2)}, u32[]{:S(2)}) %collective-permute-start.12) | collective-permute-done | bytes 245792 | tf_op jit(solution)/shard_map/ppermute | solution.py:251
  56.0 3.9 %collective-permute-done.14.refs_6_ = bf16[240,512]{1,0:T(8,128)(2,1)S(1)} collective-permute-done((bf16[240,512]{1,0:T(8,128)(2,1)S(1)}, bf16[240,512]{1,0:T(8,128)(2,1)S(1)}, u32[]{:S(2)}, u32[]{:S(2)}) %collective-permute-start.14) | collective-permute-done | bytes 245792 | tf_op jit(solution)/shard_map/ppermute | solution.py:251
  60.6 2.0 collective-permute-start.27
  64.2 2.6 %collective-permute-done.5.refs_7_ = bf16[240,512]{1,0:T(8,128)(2,1)S(1)} collective-permute-done((bf16[240,512]{1,0:T(8,128)(2,1)S(1)}, bf16[240,512]{1,0:T(8,128)(2,1)S(1)}, u32[]{:S(2)}, u32[]{:S(2)}) %collective-permute-start.5) | collective-permute-done | bytes 245792 | tf_op jit(solution)/shard_map/ppermute | solution.py:251
  68.1 4.1 %collective-permute-done.2.refs_4_ = bf16[240,512]{1,0:T(8,128)(2,1)S(1)} collective-permute-done((bf16[240,512]{1,0:T(8,128)(2,1)S(1)}, bf16[240,512]{1,0:T(8,128)(2,1)S(1)}, u32[]{:S(2)}, u32[]{:S(2)}) %collective-permute-start.2) | collective-permute-done | bytes 245792 | tf_op jit(solution)/shard_map/ppermute | solution.py:251
  73.3 4.0 %collective-permute-done.4.refs_6_ = bf16[240,512]{1,0:T(8,128)(2,1)S(1)} collective-permute-done((bf16[240,512]{1,0:T(8,128)(2,1)S(1)}, bf16[240,512]{1,0:T(8,128)(2,1)S(1)}, u32[]{:S(2)}, u32[]{:S(2)}) %collective-permute-start.4) | collective-permute-done | bytes 245792 | tf_op jit(solution)/shard_map/ppermute | solution.py:251
  80.0 5.4 %collective-permute-done.27.refs_2_ = bf16[480,512]{1,0:T(8,128)(2,1)} collective-permute-done((bf16[480,512]{1,0:T(8,128)(2,1)S(1)}, bf16[480,512]{1,0:T(8,128)(2,1)}, u32[]{:S(2)}, u32[]{:S(2)}) %collective-permute-start.27) | collective-permute-done | bytes 491552 | tf_op jit(solution)/shard_map/ppermute | solution.py:237
  85.4 10.5 %collective-permute-done.24.refs_2_ = bf16[480,512]{1,0:T(8,128)(2,1)} collective-permute-done((bf16[480,512]{1,0:T(8,128)(2,1)S(1)}, bf16[480,512]{1,0:T(8,128)(2,1)}, u32[]{:S(2)}, u32[]{:S(2)}) %collective-permute-start.24) | collective-permute-done | bytes 491552 | tf_op jit(solution)/shard_map/ppermute | solution.py:237
  96.6 9.8 %collective-permute-done.21.refs_2_ = bf16[480,512]{1,0:T(8,128)(2,1)} collective-permute-done((bf16[480,512]{1,0:T(8,128)(2,1)S(1)}, bf16[480,512]{1,0:T(8,128)(2,1)}, u32[]{:S(2)}, u32[]{:S(2)}) %collective-permute-start.21) | collective-permute-done | bytes 491552 | tf_op jit(solution)/shard_map/ppermute | solution.py:237
  107.2 9.6 %collective-permute-done.18.refs_2_ = bf16[480,512]{1,0:T(8,128)(2,1)S(1)} collective-permute-done((bf16[480,512]{1,0:T(8,128)(2,1)S(1)}, bf16[480,512]{1,0:T(8,128)(2,1)S(1)}, u32[]{:S(2)}, u32[]{:S(2)}) %collective-permute-start.18) | collective-permute-done | bytes 491552 | tf_op jit(solution)/shard_map/ppermute | solution.py:237
  116.9 8.6 %collective-permute-done.8.refs_2_ = bf16[480,512]{1,0:T(8,128)(2,1)S(1)} collective-permute-done((bf16[480,512]{1,0:T(8,128)(2,1)S(1)}, bf16[480,512]{1,0:T(8,128)(2,1)S(1)}, u32[]{:S(2)}, u32[]{:S(2)}) %collective-permute-start.8) | collective-permute-done | bytes 491552 | tf_op jit(solution)/shard_map/ppermute | solution.py:237
  126.8 4.8 %collective-permute-done.6.refs_8_ = bf16[240,512]{1,0:T(8,128)(2,1)S(1)} collective-permute-done((bf16[240,512]{1,0:T(8,128)(2,1)S(1)}, bf16[240,512]{1,0:T(8,128)(2,1)S(1)}, u32[]{:S(2)}, u32[]{:S(2)}) %collective-permute-start.6) | collective-permute-done | bytes 245792 | tf_op jit(solution)/shard_map/ppermute | solution.py:251
  141.4 3.8 %assemble.3.tok = bf16[512,1920]{1,0:T(8,128)(2,1)S(1)} custom-call(s32[2]{0:T(128)S(1)} %pad_add_fusion.refs_0_, bf16[240,512]{1,0:T(8,128)(2,1)S(1)} %copy-done.15, bf16[240,512]{1,0:T(8,128)(2,1)S(1)} %copy-done.27, bf16[240,512]{1,0:T(8,128)(2,1)S(1)} %copy-done.25, bf16[240,512]{1,0:T(8,128)(2,1)S(1)} %copy-done.33, bf16[240,512]{1,0:T(8,128)(2,1)S(1)} %copy-done.23, ...), custom_call_target="tpu_custom_call" | custom-call | tf_op jit(solution)/shard_map/assemble/pallas_call | solution.py:44
  145.7 2.1 send_part.13
  147.9 1.6 collective-permute-start.36
  149.4 3.2 %send_part.12 = bf16[512,512]{1,0:T(8,128)(2,1)} custom-call(bf16[512,1920]{1,0:T(8,128)(2,1)S(1)} %assemble.3.tok, bf16[480,3072]{1,0:T(8,128)(2,1)S(1)} %copy-done, bf16[480,3072]{1,0:T(8,128)(2,1)S(1)} %collective-permute-done.7.refs_1_, bf16[480,512]{1,0:T(8,128)(2,1)} %collective-permute-done.30.refs_2_, bf16[480,512]{1,0:T(8,128)(2,1)} %collective-permute-done.31.refs_3_), custom_call_target="tpu_custom_call" | custom-call | flops 1006632960 | bytes 1966080 | tf_op jit(solution)/shard_map/send_part/pallas_call | solution.py:107
  153.4 3.9 %assemble.2.tok = bf16[512,1920]{1,0:T(8,128)(2,1)S(1)} custom-call(s32[2]{0:T(128)S(1)} %pad_add_fusion.refs_0_, bf16[240,512]{1,0:T(8,128)(2,1)S(1)} %copy-done.13, bf16[240,512]{1,0:T(8,128)(2,1)S(1)} %copy-done.21, bf16[240,512]{1,0:T(8,128)(2,1)S(1)} %copy-done.19, bf16[240,512]{1,0:T(8,128)(2,1)S(1)} %copy-done.35, bf16[240,512]{1,0:T(8,128)(2,1)S(1)} %copy-done.17, ...), custom_call_target="tpu_custom_call" | custom-call | tf_op jit(solution)/shard_map/assemble/pallas_call | solution.py:44
  157.3 3.2 %send_part.11 = bf16[512,512]{1,0:T(8,128)(2,1)} custom-call(bf16[512,1920]{1,0:T(8,128)(2,1)S(1)} %assemble.3.tok, bf16[480,3072]{1,0:T(8,128)(2,1)S(1)} %copy-done, bf16[480,3072]{1,0:T(8,128)(2,1)S(1)} %collective-permute-done.7.refs_1_, bf16[480,512]{1,0:T(8,128)(2,1)} %collective-permute-done.27.refs_2_, bf16[480,512]{1,0:T(8,128)(2,1)} %collective-permute-done.28.refs_3_), custom_call_target="tpu_custom_call" | custom-call | flops 1006632960 | bytes 1966080 | tf_op jit(solution)/shard_map/send_part/pallas_call | solution.py:107
  160.6 1.5 collective-permute-start.29
  162.1 3.3 %send_part.10 = bf16[512,512]{1,0:T(8,128)(2,1)} custom-call(bf16[512,1920]{1,0:T(8,128)(2,1)S(1)} %assemble.3.tok, bf16[480,3072]{1,0:T(8,128)(2,1)S(1)} %copy-done, bf16[480,3072]{1,0:T(8,128)(2,1)S(1)} %collective-permute-done.7.refs_1_, bf16[480,512]{1,0:T(8,128)(2,1)} %collective-permute-done.24.refs_2_, bf16[480,512]{1,0:T(8,128)(2,1)} %collective-permute-done.25.refs_3_), custom_call_target="tpu_custom_call" | custom-call | flops 1006632960 | bytes 1966080 | tf_op jit(solution)/shard_map/send_part/pallas_call | solution.py:107
  166.1 3.3 %send_part.9 = bf16[512,512]{1,0:T(8,128)(2,1)} custom-call(bf16[512,1920]{1,0:T(8,128)(2,1)S(1)} %assemble.3.tok, bf16[480,3072]{1,0:T(8,128)(2,1)S(1)} %copy-done, bf16[480,3072]{1,0:T(8,128)(2,1)S(1)} %collective-permute-done.7.refs_1_, bf16[480,512]{1,0:T(8,128)(2,1)} %collective-permute-done.21.refs_2_, bf16[480,512]{1,0:T(8,128)(2,1)} %collective-permute-done.22.refs_3_), custom_call_target="tpu_custom_call" | custom-call | flops 1006632960 | bytes 1966080 | tf_op jit(solution)/shard_map/send_part/pallas_call | solution.py:107
  169.4 1.5 collective-permute-start.23
  170.9 2.1 send_part.8
  173.6 2.1 send_part.7
  175.7 1.5 collective-permute-start.17
  177.2 2.1 keep_part.7.refs_5_
  179.3 3.2 %keep_part.8.refs_5_ = bf16[512,3584]{1,0:T(8,128)(2,1)} custom-call(bf16[512,1920]{1,0:T(8,128)(2,1)S(1)} %assemble.2.tok, bf16[480,3072]{1,0:T(8,128)(2,1)S(1)} %copy-done, bf16[480,3072]{1,0:T(8,128)(2,1)S(1)} %collective-permute-done.7.refs_1_, bf16[480,512]{1,0:T(8,128)(2,1)} %collective-permute-done.30.refs_2_, ...), custom_call_target="tpu_custom_call", output_to_operand_aliasing={{}: (6, {})} | custom-call | flops 1006632960 | bytes 1966080 | tf_op jit(solution)/shard_map/keep_part/pallas_call | solution.py:127
  182.5 2.9 %collective-permute-done.29.refs_4_ = bf16[512,512]{1,0:T(8,128)(2,1)S(1)} collective-permute-done((bf16[512,512]{1,0:T(8,128)(2,1)}, bf16[512,512]{1,0:T(8,128)(2,1)S(1)}, u32[]{:S(2)}, u32[]{:S(2)}) %collective-permute-start.29) | collective-permute-done | bytes 524320 | tf_op jit(solution)/shard_map/ppermute | solution.py:241
  185.4 3.2 %keep_part.9.refs_5_ = bf16[512,3584]{1,0:T(8,128)(2,1)} custom-call(bf16[512,1920]{1,0:T(8,128)(2,1)S(1)} %assemble.2.tok, bf16[480,3072]{1,0:T(8,128)(2,1)S(1)} %copy-done, bf16[480,3072]{1,0:T(8,128)(2,1)S(1)} %collective-permute-done.7.refs_1_, bf16[480,512]{1,0:T(8,128)(2,1)} %collective-permute-done.27.refs_2_, ...), custom_call_target="tpu_custom_call", output_to_operand_aliasing={{}: (6, {})} | custom-call | flops 1006632960 | bytes 1966080 | tf_op jit(solution)/shard_map/keep_part/pallas_call | solution.py:127
  188.7 8.0 %collective-permute-done.26.refs_4_ = bf16[512,512]{1,0:T(8,128)(2,1)S(1)} collective-permute-done((bf16[512,512]{1,0:T(8,128)(2,1)}, bf16[512,512]{1,0:T(8,128)(2,1)S(1)}, u32[]{:S(2)}, u32[]{:S(2)}) %collective-permute-start.26) | collective-permute-done | bytes 524320 | tf_op jit(solution)/shard_map/ppermute | solution.py:241
  196.7 3.2 %keep_part.10.refs_5_ = bf16[512,3584]{1,0:T(8,128)(2,1)} custom-call(bf16[512,1920]{1,0:T(8,128)(2,1)S(1)} %assemble.2.tok, bf16[480,3072]{1,0:T(8,128)(2,1)S(1)} %copy-done, bf16[480,3072]{1,0:T(8,128)(2,1)S(1)} %collective-permute-done.7.refs_1_, bf16[480,512]{1,0:T(8,128)(2,1)} %collective-permute-done.24.refs_2_, ...), custom_call_target="tpu_custom_call", output_to_operand_aliasing={{}: (6, {})} | custom-call | flops 1006632960 | bytes 1966080 | tf_op jit(solution)/shard_map/keep_part/pallas_call | solution.py:127
  199.9 8.0 %collective-permute-done.23.refs_4_ = bf16[512,512]{1,0:T(8,128)(2,1)S(1)} collective-permute-done((bf16[512,512]{1,0:T(8,128)(2,1)}, bf16[512,512]{1,0:T(8,128)(2,1)S(1)}, u32[]{:S(2)}, u32[]{:S(2)}) %collective-permute-start.23) | collective-permute-done | bytes 524320 | tf_op jit(solution)/shard_map/ppermute | solution.py:241
  207.9 3.2 %keep_part.11.refs_5_ = bf16[512,3584]{1,0:T(8,128)(2,1)} custom-call(bf16[512,1920]{1,0:T(8,128)(2,1)S(1)} %assemble.2.tok, bf16[480,3072]{1,0:T(8,128)(2,1)S(1)} %copy-done, bf16[480,3072]{1,0:T(8,128)(2,1)S(1)} %collective-permute-done.7.refs_1_, bf16[480,512]{1,0:T(8,128)(2,1)} %collective-permute-done.21.refs_2_, ...), custom_call_target="tpu_custom_call", output_to_operand_aliasing={{}: (6, {})} | custom-call | flops 1006632960 | bytes 1966080 | tf_op jit(solution)/shard_map/keep_part/pallas_call | solution.py:127
  211.1 8.0 %collective-permute-done.20.refs_4_ = bf16[512,512]{1,0:T(8,128)(2,1)S(1)} collective-permute-done((bf16[512,512]{1,0:T(8,128)(2,1)}, bf16[512,512]{1,0:T(8,128)(2,1)S(1)}, u32[]{:S(2)}, u32[]{:S(2)}) %collective-permute-start.20) | collective-permute-done | bytes 524320 | tf_op jit(solution)/shard_map/ppermute | solution.py:241
  219.1 2.1 keep_part.12.refs_5_
  221.2 8.3 %collective-permute-done.17.refs_4_ = bf16[512,512]{1,0:T(8,128)(2,1)S(1)} collective-permute-done((bf16[512,512]{1,0:T(8,128)(2,1)}, bf16[512,512]{1,0:T(8,128)(2,1)S(1)}, u32[]{:S(2)}, u32[]{:S(2)}) %collective-permute-start.17) | collective-permute-done | bytes 524320 | tf_op jit(solution)/shard_map/ppermute | solution.py:241
  229.5 2.1 keep_part.13
  (146 shorter events, 30.7 us)
Async XLA Ops:
  8.5 139.4 %collective-permute-start.7 = (bf16[480,3072]{1,0:T(8,128)(2,1)}, bf16[480,3072]{1,0:T(8,128)(2,1)S(1)}, u32[]{:S(2)}, u32[]{:S(2)}) collective-permute-start(bf16[480,3072]{1,0:T(8,128)(2,1)} %get-tuple-element.14.refs_0_), channel_id=1, source_target_pairs={{0,4},{4,0},{1,5},{5,1},{2,6},{6,2},{3,7},{7,3},{8,12},{12,8},{9,1... | collective-permute-start | bytes 8847368 | tf_op jit(solution)/shard_map/ppermute | solution.py:244
  10.4 25.4 %copy-start.12 = (bf16[240,512]{1,0:T(8,128)(2,1)}, bf16[240,512]{1,0:T(8,128)(2,1)S(1)}, u32[]{:S(2)}) copy-start(bf16[240,512]{1,0:T(8,128)(2,1)S(1)} %get-tuple-element.25.refs_1_) | copy-start | bytes 737284
  10.4 25.4 %copy-start.14 = (bf16[240,512]{1,0:T(8,128)(2,1)}, bf16[240,512]{1,0:T(8,128)(2,1)S(1)}, u32[]{:S(2)}) copy-start(bf16[240,512]{1,0:T(8,128)(2,1)S(1)} %get-tuple-element.26.refs_1_) | copy-start | bytes 737284
  10.4 9.4 %collective-permute-start.13 = (bf16[240,512]{1,0:T(8,128)(2,1)S(1)}, bf16[240,512]{1,0:T(8,128)(2,1)S(1)}, u32[]{:S(2)}, u32[]{:S(2)}) collective-permute-start(bf16[240,512]{1,0:T(8,128)(2,1)S(1)} %get-tuple-element.23), channel_id=1, source_target_pairs={{0,16},{8,24},{16,0},{24,8},{1,17},{9,25},{17,1},{25,9},{2,18},{10... | collective-permute-start | bytes 737288 | tf_op jit(solution)/shard_map/ppermute | solution.py:237
  13.1 15.7 %collective-permute-start.11 = (bf16[240,512]{1,0:T(8,128)(2,1)S(1)}, bf16[240,512]{1,0:T(8,128)(2,1)S(1)}, u32[]{:S(2)}, u32[]{:S(2)}) collective-permute-start(bf16[240,512]{1,0:T(8,128)(2,1)S(1)} %get-tuple-element.26.refs_1_), channel_id=1, source_target_pairs={{0,2},{1,3},{2,0},{3,1},{4,6},{5,7},{6,4},{7,5},{8,10},{9,11},{10,... | collective-permute-start | bytes 737288 | tf_op jit(solution)/shard_map/ppermute | solution.py:251
  15.7 13.2 %collective-permute-start.10 = (bf16[240,512]{1,0:T(8,128)(2,1)S(1)}, bf16[240,512]{1,0:T(8,128)(2,1)S(1)}, u32[]{:S(2)}, u32[]{:S(2)}) collective-permute-start(bf16[240,512]{1,0:T(8,128)(2,1)S(1)} %get-tuple-element.26.refs_1_), channel_id=1, source_target_pairs={{0,1},{1,0},{2,3},{3,2},{4,5},{5,4},{6,7},{7,6},{8,9},{9,8},{10,11... | collective-permute-start | bytes 737288 | tf_op jit(solution)/shard_map/ppermute | solution.py:251
  17.3 18.6 %collective-permute-start.3 = (bf16[240,512]{1,0:T(8,128)(2,1)S(1)}, bf16[240,512]{1,0:T(8,128)(2,1)S(1)}, u32[]{:S(2)}, u32[]{:S(2)}) collective-permute-start(bf16[240,512]{1,0:T(8,128)(2,1)S(1)} %get-tuple-element.24), channel_id=1, source_target_pairs={{0,16},{8,24},{16,0},{24,8},{1,17},{9,25},{17,1},{25,9},{2,18},{10... | collective-permute-start | bytes 737288 | tf_op jit(solution)/shard_map/ppermute | solution.py:237
  19.8 28.7 %copy-start.22 = (bf16[240,512]{1,0:T(8,128)(2,1)}, bf16[240,512]{1,0:T(8,128)(2,1)S(1)}, u32[]{:S(2)}) copy-start(bf16[240,512]{1,0:T(8,128)(2,1)S(1)} %collective-permute-done.13.refs_5_) | copy-start | bytes 737284
  19.8 40.8 %copy-start.49 = (bf16[480,512]{1,0:T(8,128)(2,1)S(1)}, bf16[480,512]{1,0:T(8,128)(2,1)}, u32[]{:S(2)}) copy-start(bf16[480,512]{1,0:T(8,128)(2,1)} %get-tuple-element.20) | copy-start | bytes 1474564
  19.8 40.8 %copy-start.48 = (bf16[480,512]{1,0:T(8,128)(2,1)S(1)}, bf16[480,512]{1,0:T(8,128)(2,1)}, u32[]{:S(2)}) copy-start(bf16[480,512]{1,0:T(8,128)(2,1)} %get-tuple-element.19) | copy-start | bytes 1474564
  19.8 53.1 %copy-start.47 = (bf16[480,512]{1,0:T(8,128)(2,1)S(1)}, bf16[480,512]{1,0:T(8,128)(2,1)}, u32[]{:S(2)}) copy-start(bf16[480,512]{1,0:T(8,128)(2,1)} %get-tuple-element.18) | copy-start | bytes 1474564
  19.8 58.1 %copy-start.46 = (bf16[480,512]{1,0:T(8,128)(2,1)S(1)}, bf16[480,512]{1,0:T(8,128)(2,1)}, u32[]{:S(2)}) copy-start(bf16[480,512]{1,0:T(8,128)(2,1)} %get-tuple-element.17) | copy-start | bytes 1474564
  19.8 58.6 %copy-start.45 = (bf16[480,512]{1,0:T(8,128)(2,1)S(1)}, bf16[480,512]{1,0:T(8,128)(2,1)}, u32[]{:S(2)}) copy-start(bf16[480,512]{1,0:T(8,128)(2,1)} %get-tuple-element.16) | copy-start | bytes 1474564
  19.9 65.5 %copy-start.44 = (bf16[480,512]{1,0:T(8,128)(2,1)S(1)}, bf16[480,512]{1,0:T(8,128)(2,1)}, u32[]{:S(2)}) copy-start(bf16[480,512]{1,0:T(8,128)(2,1)} %get-tuple-element.15) | copy-start | bytes 1474564
  19.9 19.6 %collective-permute-start.1 = (bf16[240,512]{1,0:T(8,128)(2,1)S(1)}, bf16[240,512]{1,0:T(8,128)(2,1)S(1)}, u32[]{:S(2)}, u32[]{:S(2)}) collective-permute-start(bf16[240,512]{1,0:T(8,128)(2,1)S(1)} %get-tuple-element.25.refs_1_), channel_id=1, source_target_pairs={{0,2},{1,3},{2,0},{3,1},{4,6},{5,7},{6,4},{7,5},{8,10},{9,11},{10,... | collective-permute-start | bytes 737288 | tf_op jit(solution)/shard_map/ppermute | solution.py:251
  28.8 11.5 %collective-permute-start = (bf16[240,512]{1,0:T(8,128)(2,1)S(1)}, bf16[240,512]{1,0:T(8,128)(2,1)S(1)}, u32[]{:S(2)}, u32[]{:S(2)}) collective-permute-start(bf16[240,512]{1,0:T(8,128)(2,1)S(1)} %get-tuple-element.25.refs_1_), channel_id=1, source_target_pairs={{0,1},{1,0},{2,3},{3,2},{4,5},{5,4},{6,7},{7,6},{8,9},{9,8},{10,11... | collective-permute-start | bytes 737288 | tf_op jit(solution)/shard_map/ppermute | solution.py:251
  29.6 18.9 %collective-permute-start.15 = (bf16[240,512]{1,0:T(8,128)(2,1)S(1)}, bf16[240,512]{1,0:T(8,128)(2,1)S(1)}, u32[]{:S(2)}, u32[]{:S(2)}) collective-permute-start(bf16[240,512]{1,0:T(8,128)(2,1)S(1)} %collective-permute-done.13.refs_5_), channel_id=1, source_target_pairs={{0,2},{1,3},{2,0},{3,1},{4,6},{5,7},{6,4},{7,5},{8,10},{9,11},{10,... | collective-permute-start | bytes 737288 | tf_op jit(solution)/shard_map/ppermute | solution.py:251
  35.9 109.8 %copy-start.1 = (bf16[480,512]{1,0:T(8,128)(2,1)S(1)}, bf16[480,512]{1,0:T(8,128)(2,1)}, u32[]{:S(2)}) copy-start(bf16[480,512]{1,0:T(8,128)(2,1)} %get-tuple-element.21.refs_0_) | copy-start | bytes 1474564
  35.9 24.7 %collective-permute-start.34 = (bf16[480,512]{1,0:T(8,128)(2,1)}, bf16[480,512]{1,0:T(8,128)(2,1)S(1)}, u32[]{:S(2)}, u32[]{:S(2)}) collective-permute-start(bf16[480,512]{1,0:T(8,128)(2,1)} %get-tuple-element.22), channel_id=1, source_target_pairs={{0,16},{8,24},{16,0},{24,8},{1,17},{9,25},{17,1},{25,9},{2,18},{10... | collective-permute-start | bytes 1474568 | tf_op jit(solution)/shard_map/ppermute | solution.py:237
  39.4 23.2 %collective-permute-start.33 = (bf16[480,512]{1,0:T(8,128)(2,1)}, bf16[480,512]{1,0:T(8,128)(2,1)S(1)}, u32[]{:S(2)}, u32[]{:S(2)}) collective-permute-start(bf16[480,512]{1,0:T(8,128)(2,1)} %get-tuple-element.21.refs_0_), channel_id=1, source_target_pairs={{0,4},{4,0},{1,5},{5,1},{2,6},{6,2},{3,7},{7,3},{8,12},{12,8},{9,1... | collective-permute-start | bytes 1474568 | tf_op jit(solution)/shard_map/ppermute | solution.py:244
  41.0 12.8 %collective-permute-start.12 = (bf16[240,512]{1,0:T(8,128)(2,1)S(1)}, bf16[240,512]{1,0:T(8,128)(2,1)S(1)}, u32[]{:S(2)}, u32[]{:S(2)}) collective-permute-start(bf16[240,512]{1,0:T(8,128)(2,1)S(1)} %collective-permute-done.11.refs_3_), channel_id=1, source_target_pairs={{0,1},{1,0},{2,3},{3,2},{4,5},{5,4},{6,7},{7,6},{8,9},{9,8},{10,11... | collective-permute-start | bytes 737288 | tf_op jit(solution)/shard_map/ppermute | solution.py:251
  48.5 11.4 %collective-permute-start.14 = (bf16[240,512]{1,0:T(8,128)(2,1)S(1)}, bf16[240,512]{1,0:T(8,128)(2,1)S(1)}, u32[]{:S(2)}, u32[]{:S(2)}) collective-permute-start(bf16[240,512]{1,0:T(8,128)(2,1)S(1)} %collective-permute-done.13.refs_5_), channel_id=1, source_target_pairs={{0,1},{1,0},{2,3},{3,2},{4,5},{5,4},{6,7},{7,6},{8,9},{9,8},{10,11... | collective-permute-start | bytes 737288 | tf_op jit(solution)/shard_map/ppermute | solution.py:251
  54.5 12.3 %collective-permute-start.5 = (bf16[240,512]{1,0:T(8,128)(2,1)S(1)}, bf16[240,512]{1,0:T(8,128)(2,1)S(1)}, u32[]{:S(2)}, u32[]{:S(2)}) collective-permute-start(bf16[240,512]{1,0:T(8,128)(2,1)S(1)} %collective-permute-done.3.refs_5_), channel_id=1, source_target_pairs={{0,2},{1,3},{2,0},{3,1},{4,6},{5,7},{6,4},{7,5},{8,10},{9,11},{10,... | collective-permute-start | bytes 737288 | tf_op jit(solution)/shard_map/ppermute | solution.py:251
  60.6 17.8 %collective-permute-start.30 = (bf16[480,512]{1,0:T(8,128)(2,1)S(1)}, bf16[480,512]{1,0:T(8,128)(2,1)}, u32[]{:S(2)}, u32[]{:S(2)}) collective-permute-start(bf16[480,512]{1,0:T(8,128)(2,1)S(1)} %copy-done.49), channel_id=1, source_target_pairs={{0,16},{8,24},{16,0},{24,8},{1,17},{9,25},{17,1},{25,9},{2,18},{10... | collective-permute-start | bytes 1474568 | tf_op jit(solution)/shard_map/ppermute | solution.py:237
  60.6 24.7 %collective-permute-start.27 = (bf16[480,512]{1,0:T(8,128)(2,1)S(1)}, bf16[480,512]{1,0:T(8,128)(2,1)}, u32[]{:S(2)}, u32[]{:S(2)}) collective-permute-start(bf16[480,512]{1,0:T(8,128)(2,1)S(1)} %copy-done.48), channel_id=1, source_target_pairs={{0,16},{8,24},{16,0},{24,8},{1,17},{9,25},{17,1},{25,9},{2,18},{10... | collective-permute-start | bytes 1474568 | tf_op jit(solution)/shard_map/ppermute | solution.py:237
  63.4 8.8 %collective-permute-start.2 = (bf16[240,512]{1,0:T(8,128)(2,1)S(1)}, bf16[240,512]{1,0:T(8,128)(2,1)S(1)}, u32[]{:S(2)}, u32[]{:S(2)}) collective-permute-start(bf16[240,512]{1,0:T(8,128)(2,1)S(1)} %collective-permute-done.1.refs_3_), channel_id=1, source_target_pairs={{0,1},{1,0},{2,3},{3,2},{4,5},{5,4},{6,7},{7,6},{8,9},{9,8},{10,11... | collective-permute-start | bytes 737288 | tf_op jit(solution)/shard_map/ppermute | solution.py:251
  66.8 10.4 %collective-permute-start.4 = (bf16[240,512]{1,0:T(8,128)(2,1)S(1)}, bf16[240,512]{1,0:T(8,128)(2,1)S(1)}, u32[]{:S(2)}, u32[]{:S(2)}) collective-permute-start(bf16[240,512]{1,0:T(8,128)(2,1)S(1)} %collective-permute-done.3.refs_5_), channel_id=1, source_target_pairs={{0,1},{1,0},{2,3},{3,2},{4,5},{5,4},{6,7},{7,6},{8,9},{9,8},{10,11... | collective-permute-start | bytes 737288 | tf_op jit(solution)/shard_map/ppermute | solution.py:251
  73.0 22.9 %collective-permute-start.24 = (bf16[480,512]{1,0:T(8,128)(2,1)S(1)}, bf16[480,512]{1,0:T(8,128)(2,1)}, u32[]{:S(2)}, u32[]{:S(2)}) collective-permute-start(bf16[480,512]{1,0:T(8,128)(2,1)S(1)} %copy-done.47), channel_id=1, source_target_pairs={{0,16},{8,24},{16,0},{24,8},{1,17},{9,25},{17,1},{25,9},{2,18},{10... | collective-permute-start | bytes 1474568 | tf_op jit(solution)/shard_map/ppermute | solution.py:237
  77.9 28.5 %collective-permute-start.21 = (bf16[480,512]{1,0:T(8,128)(2,1)S(1)}, bf16[480,512]{1,0:T(8,128)(2,1)}, u32[]{:S(2)}, u32[]{:S(2)}) collective-permute-start(bf16[480,512]{1,0:T(8,128)(2,1)S(1)} %copy-done.46), channel_id=1, source_target_pairs={{0,16},{8,24},{16,0},{24,8},{1,17},{9,25},{17,1},{25,9},{2,18},{10... | collective-permute-start | bytes 1474568 | tf_op jit(solution)/shard_map/ppermute | solution.py:237
  78.5 38.4 %collective-permute-start.18 = (bf16[480,512]{1,0:T(8,128)(2,1)S(1)}, bf16[480,512]{1,0:T(8,128)(2,1)S(1)}, u32[]{:S(2)}, u32[]{:S(2)}) collective-permute-start(bf16[480,512]{1,0:T(8,128)(2,1)S(1)} %copy-done.45), channel_id=1, source_target_pairs={{0,16},{8,24},{16,0},{24,8},{1,17},{9,25},{17,1},{25,9},{2,18},{10... | collective-permute-start | bytes 1474568 | tf_op jit(solution)/shard_map/ppermute | solution.py:237
  85.4 40.0 %collective-permute-start.8 = (bf16[480,512]{1,0:T(8,128)(2,1)S(1)}, bf16[480,512]{1,0:T(8,128)(2,1)S(1)}, u32[]{:S(2)}, u32[]{:S(2)}) collective-permute-start(bf16[480,512]{1,0:T(8,128)(2,1)S(1)} %copy-done.44), channel_id=1, source_target_pairs={{0,16},{8,24},{16,0},{24,8},{1,17},{9,25},{17,1},{25,9},{2,18},{10... | collective-permute-start | bytes 1474568 | tf_op jit(solution)/shard_map/ppermute | solution.py:237
  95.9 30.3 %collective-permute-start.16 = (bf16[240,512]{1,0:T(8,128)(2,1)S(1)}, bf16[240,512]{1,0:T(8,128)(2,1)S(1)}, u32[]{:S(2)}, u32[]{:S(2)}) collective-permute-start(bf16[240,512]{1,0:T(8,128)(2,1)S(1)} %collective-permute-done.15.refs_7_), channel_id=1, source_target_pairs={{0,1},{1,0},{2,3},{3,2},{4,5},{5,4},{6,7},{7,6},{8,9},{9,8},{10,11... | collective-permute-start | bytes 737288 | tf_op jit(solution)/shard_map/ppermute | solution.py:251
  106.4 25.9 %collective-permute-start.35 = (bf16[480,512]{1,0:T(8,128)(2,1)S(1)}, bf16[480,512]{1,0:T(8,128)(2,1)S(1)}, u32[]{:S(2)}, u32[]{:S(2)}) collective-permute-start(bf16[480,512]{1,0:T(8,128)(2,1)S(1)} %collective-permute-done.34.refs_2_), channel_id=1, source_target_pairs={{0,4},{4,0},{1,5},{5,1},{2,6},{6,2},{3,7},{7,3},{8,12},{12,8},{9,1... | collective-permute-start | bytes 1474568 | tf_op jit(solution)/shard_map/ppermute | solution.py:244
  116.8 15.5 %copy-start.8 = (bf16[480,512]{1,0:T(8,128)(2,1)}, bf16[480,512]{1,0:T(8,128)(2,1)S(1)}, u32[]{:S(2)}) copy-start(bf16[480,512]{1,0:T(8,128)(2,1)S(1)} %collective-permute-done.18.refs_2_) | copy-start | bytes 1474564
  116.9 16.8 %collective-permute-start.31 = (bf16[480,512]{1,0:T(8,128)(2,1)}, bf16[480,512]{1,0:T(8,128)(2,1)}, u32[]{:S(2)}, u32[]{:S(2)}) collective-permute-start(bf16[480,512]{1,0:T(8,128)(2,1)} %collective-permute-done.30.refs_2_), channel_id=1, source_target_pairs={{0,4},{4,0},{1,5},{5,1},{2,6},{6,2},{3,7},{7,3},{8,12},{12,8},{9,1... | collective-permute-start | bytes 1474568 | tf_op jit(solution)/shard_map/ppermute | solution.py:244
  125.4 6.2 %collective-permute-start.6 = (bf16[240,512]{1,0:T(8,128)(2,1)S(1)}, bf16[240,512]{1,0:T(8,128)(2,1)S(1)}, u32[]{:S(2)}, u32[]{:S(2)}) collective-permute-start(bf16[240,512]{1,0:T(8,128)(2,1)S(1)} %collective-permute-done.5.refs_7_), channel_id=1, source_target_pairs={{0,1},{1,0},{2,3},{3,2},{4,5},{5,4},{6,7},{7,6},{8,9},{9,8},{10,11... | collective-permute-start | bytes 737288 | tf_op jit(solution)/shard_map/ppermute | solution.py:251
  126.8 18.4 %collective-permute-start.28 = (bf16[480,512]{1,0:T(8,128)(2,1)}, bf16[480,512]{1,0:T(8,128)(2,1)}, u32[]{:S(2)}, u32[]{:S(2)}) collective-permute-start(bf16[480,512]{1,0:T(8,128)(2,1)} %collective-permute-done.27.refs_2_), channel_id=1, source_target_pairs={{0,4},{4,0},{1,5},{5,1},{2,6},{6,2},{3,7},{7,3},{8,12},{12,8},{9,1... | collective-permute-start | bytes 1474568 | tf_op jit(solution)/shard_map/ppermute | solution.py:244
  132.3 20.4 %collective-permute-start.25 = (bf16[480,512]{1,0:T(8,128)(2,1)}, bf16[480,512]{1,0:T(8,128)(2,1)}, u32[]{:S(2)}, u32[]{:S(2)}) collective-permute-start(bf16[480,512]{1,0:T(8,128)(2,1)} %collective-permute-done.24.refs_2_), channel_id=1, source_target_pairs={{0,4},{4,0},{1,5},{5,1},{2,6},{6,2},{3,7},{7,3},{8,12},{12,8},{9,1... | collective-permute-start | bytes 1474568 | tf_op jit(solution)/shard_map/ppermute | solution.py:244
  133.1 27.5 %collective-permute-start.22 = (bf16[480,512]{1,0:T(8,128)(2,1)}, bf16[480,512]{1,0:T(8,128)(2,1)}, u32[]{:S(2)}, u32[]{:S(2)}) collective-permute-start(bf16[480,512]{1,0:T(8,128)(2,1)} %collective-permute-done.21.refs_2_), channel_id=1, source_target_pairs={{0,4},{4,0},{1,5},{5,1},{2,6},{6,2},{3,7},{7,3},{8,12},{12,8},{9,1... | collective-permute-start | bytes 1474568 | tf_op jit(solution)/shard_map/ppermute | solution.py:244
  133.6 31.8 %collective-permute-start.19 = (bf16[480,512]{1,0:T(8,128)(2,1)}, bf16[480,512]{1,0:T(8,128)(2,1)S(1)}, u32[]{:S(2)}, u32[]{:S(2)}) collective-permute-start(bf16[480,512]{1,0:T(8,128)(2,1)} %copy-done.8), channel_id=1, source_target_pairs={{0,4},{4,0},{1,5},{5,1},{2,6},{6,2},{3,7},{7,3},{8,12},{12,8},{9,1... | collective-permute-start | bytes 1474568 | tf_op jit(solution)/shard_map/ppermute | solution.py:244
  145.2 24.1 %collective-permute-start.9 = (bf16[480,512]{1,0:T(8,128)(2,1)S(1)}, bf16[480,512]{1,0:T(8,128)(2,1)S(1)}, u32[]{:S(2)}, u32[]{:S(2)}) collective-permute-start(bf16[480,512]{1,0:T(8,128)(2,1)S(1)} %copy-done.7), channel_id=1, source_target_pairs={{0,4},{4,0},{1,5},{5,1},{2,6},{6,2},{3,7},{7,3},{8,12},{12,8},{9,1... | collective-permute-start | bytes 1474568 | tf_op jit(solution)/shard_map/ppermute | solution.py:244
  147.9 25.1 %collective-permute-start.36 = (bf16[512,512]{1,0:T(8,128)(2,1)}, bf16[512,512]{1,0:T(8,128)(2,1)S(1)}, u32[]{:S(2)}, u32[]{:S(2)}) collective-permute-start(bf16[512,512]{1,0:T(8,128)(2,1)} %send_part.13), channel_id=1, source_target_pairs={{0,8},{8,0},{16,24},{24,16},{1,9},{9,1},{17,25},{25,17},{2,10},{10... | collective-permute-start | bytes 1572872 | tf_op jit(solution)/shard_map/ppermute | solution.py:241
  152.7 23.0 %collective-permute-start.32 = (bf16[512,512]{1,0:T(8,128)(2,1)}, bf16[512,512]{1,0:T(8,128)(2,1)S(1)}, u32[]{:S(2)}, u32[]{:S(2)}) collective-permute-start(bf16[512,512]{1,0:T(8,128)(2,1)} %send_part.12), channel_id=1, source_target_pairs={{0,8},{8,0},{16,24},{24,16},{1,9},{9,1},{17,25},{25,17},{2,10},{10... | collective-permute-start | bytes 1572872 | tf_op jit(solution)/shard_map/ppermute | solution.py:241
  160.6 24.8 %collective-permute-start.29 = (bf16[512,512]{1,0:T(8,128)(2,1)}, bf16[512,512]{1,0:T(8,128)(2,1)S(1)}, u32[]{:S(2)}, u32[]{:S(2)}) collective-permute-start(bf16[512,512]{1,0:T(8,128)(2,1)} %send_part.11), channel_id=1, source_target_pairs={{0,8},{8,0},{16,24},{24,16},{1,9},{9,1},{17,25},{25,17},{2,10},{10... | collective-permute-start | bytes 1572872 | tf_op jit(solution)/shard_map/ppermute | solution.py:241
  165.5 31.2 %collective-permute-start.26 = (bf16[512,512]{1,0:T(8,128)(2,1)}, bf16[512,512]{1,0:T(8,128)(2,1)S(1)}, u32[]{:S(2)}, u32[]{:S(2)}) collective-permute-start(bf16[512,512]{1,0:T(8,128)(2,1)} %send_part.10), channel_id=1, source_target_pairs={{0,8},{8,0},{16,24},{24,16},{1,9},{9,1},{17,25},{25,17},{2,10},{10... | collective-permute-start | bytes 1572872 | tf_op jit(solution)/shard_map/ppermute | solution.py:241
  169.4 38.5 %collective-permute-start.23 = (bf16[512,512]{1,0:T(8,128)(2,1)}, bf16[512,512]{1,0:T(8,128)(2,1)S(1)}, u32[]{:S(2)}, u32[]{:S(2)}) collective-permute-start(bf16[512,512]{1,0:T(8,128)(2,1)} %send_part.9), channel_id=1, source_target_pairs={{0,8},{8,0},{16,24},{24,16},{1,9},{9,1},{17,25},{25,17},{2,10},{10... | collective-permute-start | bytes 1572872 | tf_op jit(solution)/shard_map/ppermute | solution.py:241
  173.0 46.2 %collective-permute-start.20 = (bf16[512,512]{1,0:T(8,128)(2,1)}, bf16[512,512]{1,0:T(8,128)(2,1)S(1)}, u32[]{:S(2)}, u32[]{:S(2)}) collective-permute-start(bf16[512,512]{1,0:T(8,128)(2,1)} %send_part.8), channel_id=1, source_target_pairs={{0,8},{8,0},{16,24},{24,16},{1,9},{9,1},{17,25},{25,17},{2,10},{10... | collective-permute-start | bytes 1572872 | tf_op jit(solution)/shard_map/ppermute | solution.py:241
  175.7 53.8 %collective-permute-start.17 = (bf16[512,512]{1,0:T(8,128)(2,1)}, bf16[512,512]{1,0:T(8,128)(2,1)S(1)}, u32[]{:S(2)}, u32[]{:S(2)}) collective-permute-start(bf16[512,512]{1,0:T(8,128)(2,1)} %send_part.7), channel_id=1, source_target_pairs={{0,8},{8,0},{16,24},{24,16},{1,9},{9,1},{17,25},{25,17},{2,10},{10... | collective-permute-start | bytes 1572872 | tf_op jit(solution)/shard_map/ppermute | solution.py:241
  (39 other events, 142.3 us)
